TPU v7x, 512 devices: a 4x2x32 block of a 4x16x32 slice. The times are simulated.
512 devices in a mesh: groups: 2 (over y), band: 64 (over z, core), chan: 4 (over x).
Axes of the slice: x: 4, y: 2, z: 32, core: 2. Of those that a mesh axis runs over, the one named last changes fastest.
The devices are a block of a 4x16x32 slice.
Arguments:
- slide_region: float32 [16, 512, 8192], P('chan', ('groups', 'band')), parts along dimension 1, may hold values from -6 to 6
- row_taps: float32 [16, 257], P('chan'), may hold values from -0.375 to 0.375
- column_taps: float32 [16, 257], replicated, may hold values from -0.375 to 0.375
- channel_mix: float32 [16, 16], replicated, may hold values from -1.5 to 1.5
Outputs:
- filtered: float32 [16, 512, 8192], P('chan', ('groups', 'band')), parts along dimension 1
There are 2 independent parts, one for each index of `groups`. A program takes and returns all parts, laid end to end along the dimension named above; an argument that names none is the same for every part. Nothing has to cross between parts.
All inputs are finite; a program needn't handle non-finite values.
Results may differ from a plain program's by a relative error of at most 0.00007.
Values sent between devices are 32-bit elements; how exact they have to be, the bound alone decides.
No kernel may reach another device: no remote copies, remote signals or barrier semaphores. Data moves between devices by JAX's collectives and lax.ppermute only.
A program may use at most 64 MiB of HBM per device.

v0:
```python
import jax
import jax.numpy as jnp
from jax import lax
from jax.sharding import Mesh
from jax.sharding import PartitionSpec as P

BAND = ("band_0", "band_1")
GROUPS_BAND = ("groups", "band_0", "band_1")


precise = lax.Precision.HIGHEST


def cut_along(value, dim, size):
    before, after = (value.shape[:dim], value.shape[dim + 1 :])
    return jnp.moveaxis(value.reshape(*before, size, -1, *after), dim, 0)


def joined_along(parts, dim):
    shape = list(parts.shape[1:])
    shape[dim] *= parts.shape[0]
    return jnp.moveaxis(parts, 0, dim).reshape(shape)


def moved_by_axis(parts, axes, sequence):
    shape = [lax.axis_size(a) for a in axes]
    parts = parts.reshape(*shape, *parts.shape[1:])
    for k in sequence:
        parts = lax.all_to_all(parts, axes[k], split_axis=k, concat_axis=k, tiled=True)
    return parts.reshape(-1, *parts.shape[len(axes) :])


def core_and_chips(value, groups, sequence, split_dim, concat_dim):
    size = lax.axis_size(groups[0]) * lax.axis_size(groups[1])
    parts = cut_along(value, split_dim, size)
    return joined_along(moved_by_axis(parts, groups, sequence), concat_dim)


def sent_to_all(value, axis):
    size = lax.axis_size(axis)
    return lax.all_to_all(
        jnp.broadcast_to(value[None], (size, *value.shape)), axis, 0, 0, tiled=True
    )


def gathered_copies(value, axis, dim):
    return joined_along(sent_to_all(value, axis), dim)


def band_tables(filter_taps, tile_size):
    channels, length = filter_taps.shape
    margin = (length - 1) // 2
    period = 4 * tile_size
    border = 3 * tile_size + length
    widened = jnp.pad(filter_taps, ((0, 0), (border, border)))
    lowest = margin - tile_size + border
    window = widened[:, lowest : lowest + 3 * tile_size]
    vector = jnp.pad(window, ((0, 0), (0, tile_size)))
    repeated = jnp.tile(vector, (1, tile_size))[:, : tile_size * (period - 1)]
    toeplitz = repeated.reshape(channels, tile_size, period - 1)[:, :, : 3 * tile_size]
    stacked = jnp.transpose(toeplitz, (0, 2, 1))
    return stacked.reshape(channels, 3, tile_size, tile_size)


def along_columns(signal, filter_taps):
    tile_size = 128
    tables = band_tables(filter_taps, tile_size)
    channels, row_count, col_count = signal.shape
    tile_count = col_count // tile_size
    tiled = signal.reshape(channels, row_count, tile_count, tile_size)
    padded = jnp.pad(tiled, ((0, 0), (0, 0), (1, 1), (0, 0)))
    result = jnp.einsum(
        "crti,cij->crtj", padded[:, :, 0:tile_count], tables[:, 0], precision=precise
    )
    result = result + jnp.einsum(
        "crti,cij->crtj", padded[:, :, 1 : tile_count + 1], tables[:, 1], precision=precise
    )
    result = result + jnp.einsum(
        "crti,cij->crtj", padded[:, :, 2:], tables[:, 2], precision=precise
    )
    return result.reshape(channels, row_count, col_count)


def along_rows(signal, filter_taps):
    channels, row_count, col_count = signal.shape
    tile_size = 128
    tables = band_tables(filter_taps, tile_size)
    tile_count = row_count // tile_size
    tiled = signal.reshape(channels, tile_count, tile_size, col_count)
    padded = jnp.pad(tiled, ((0, 0), (1, 1), (0, 0), (0, 0)))
    result = jnp.einsum("ctiw,cij->ctjw", padded[:, 0:tile_count], tables[:, 0], precision=precise)
    result = result + jnp.einsum(
        "ctiw,cij->ctjw", padded[:, 1 : tile_count + 1], tables[:, 1], precision=precise
    )
    result = result + jnp.einsum("ctiw,cij->ctjw", padded[:, 2:], tables[:, 2], precision=precise)
    return result.reshape(channels, row_count, col_count)


def on_device(slide_region, row_taps, column_taps, channel_mix):
    local_channels = slide_region.shape[0]
    across = along_columns(slide_region, row_taps)
    column_band = core_and_chips(across, ("band_0", "band_1"), (1, 0), 2, 1)
    first_channel = lax.axis_index("chan") * local_channels
    own_taps = lax.dynamic_slice_in_dim(column_taps, first_channel, local_channels, 0)
    vertical = along_rows(column_band, own_taps)
    own_mixing = lax.dynamic_slice_in_dim(channel_mix, first_channel, local_channels, 0)
    blended = jnp.einsum(
        "oc,chw->ohw", own_mixing, gathered_copies(vertical, "chan", 0), precision=precise
    )
    return lax.all_to_all(blended, BAND, split_axis=1, concat_axis=2, tiled=True)


def solution(mesh):
    split = Mesh(
        mesh.devices.reshape(mesh.shape["groups"], 32, 2, mesh.shape["chan"]),
        ("groups", "band_0", "band_1", "chan"),
    )
    in_specs = (P("chan", GROUPS_BAND, None), P("chan", None), P(), P())
    out_specs = P("chan", GROUPS_BAND, None)
    return jax.shard_map(
        on_device, mesh=split, in_specs=in_specs, out_specs=out_specs, check_vma=False
    )
```

profile of v0, /device:TPU:33, one launch (start us, length us, event | category | flops | bytes accessed | tf_op | source)
XLA Modules:
  0.0 227.7 jit_solution(11120295280329860627)
XLA Ops:
  0.0 0.7 pad_slice_fusion.8
  0.7 1.4 reshape.35
  2.1 0.1 broadcast_bitcast_fusion
  2.2 0.7 copy.60
  3.0 1.0 reshape.36
  4.0 0.1 slice_bitcast_fusion
  4.1 0.3 copy.34
  4.4 0.6 convolution_bitcast_fusion.1
  5.0 0.6 convolution_bitcast_fusion
  5.6 0.6 fusion.1
  6.3 45.2 %all_to_all.33 = f32[32,2,4,4,128]{4,0,3,2,1:T(8,128)S(1)} all-to-all(f32[32,2,4,4,128]{4,0,3,2,1:T(8,128)S(1)} %copy.38), channel_id=1, replica_groups=mesh['groups'=2,'band_0'=32,'band_1'=2,'chan'=4] {'band_1'}, dimensions={1} | all-to-all | bytes 1048576 | tf_op jit(solution)/shard_map/all_to_all | solution.py:29
  51.5 1.2 copy.39
  52.7 5.5 %all-to-all-start.1 = ((f32[32,2,4,4,128]{4,1,3,2,0:T(2,128)}), f32[32,2,4,4,128]{4,1,3,2,0:T(2,128)S(1)}, u32[]{:S(2)}, u32[]{:S(2)}) async-start(f32[32,2,4,4,128]{4,1,3,2,0:T(2,128)} %copy.39), calls=%async_computation.1 | async-start | bytes 1048576 | tf_op jit(solution)/shard_map/all_to_all | solution.py:29
  58.3 0.1 broadcast_bitcast_fusion.1
  58.4 0.7 copy.59
  59.1 0.1 slice.66
  59.2 1.0 reshape.33
  60.3 0.3 copy.32
  60.5 61.6 %all-to-all-done.1 = f32[32,2,4,4,128]{4,1,3,2,0:T(2,128)S(1)} async-done(((f32[32,2,4,4,128]{4,1,3,2,0:T(2,128)}), f32[32,2,4,4,128]{4,1,3,2,0:T(2,128)S(1)}, u32[]{:S(2)}, u32[]{:S(2)}) %all-to-all-start.1) | async-done | bytes 524320 | tf_op jit(solution)/shard_map/all_to_all | solution.py:29
  122.1 0.3 copy.40
  122.4 0.3 copy.41
  122.7 0.6 fusion.2
  123.4 0.6 convolution_add_fusion.1
  124.0 0.6 convolution_add_fusion
  124.6 0.3 copy.44
  125.0 0.3 broadcast_in_dim.8
  125.3 28.8 %all_to_all.34 = f32[4,4,256,128]{3,1,2,0:T(4,128)S(1)} all-to-all(f32[4,4,256,128]{3,1,2,0:T(4,128)S(1)} %broadcast_in_dim.8), channel_id=1, replica_groups=mesh['groups'=2,'band_0'=32,'band_1'=2,'chan'=4] {'chan'}, dimensions={0} | all-to-all | bytes 4194304 | tf_op jit(solution)/shard_map/all_to_all | solution.py:41
  154.1 0.4 copy.45
  154.5 1.8 fusion.3
  156.3 70.2 %all_to_all.35 = f32[4,256,128]{2,0,1:T(4,128)S(1)} all-to-all(f32[4,256,128]{2,0,1:T(4,128)S(1)} %fusion.3), channel_id=1, replica_groups=mesh['groups'=2,'band_0'=32,'band_1'=2,'chan'=4] {'band_0','band_1'}, dimensions={1} | all-to-all | bytes 1048576 | tf_op jit(solution)/shard_map/all_to_all | solution.py:110
  226.5 0.2 copy.46
  226.6 1.0 all_to_all.28
  (9 shorter events, 0.2 us)
Async XLA Ops:
  0.0 58.2 %copy-start = (f32[16,257]{1,0:T(8,128)S(1)}, f32[16,257]{1,0:T(8,128)}, u32[]{:S(2)}) copy-start(f32[16,257]{1,0:T(8,128)} %param.6) | copy-start | bytes 49348
  52.7 69.4 %all-to-all-start.1 = ((f32[32,2,4,4,128]{4,1,3,2,0:T(2,128)}), f32[32,2,4,4,128]{4,1,3,2,0:T(2,128)S(1)}, u32[]{:S(2)}, u32[]{:S(2)}) async-start(f32[32,2,4,4,128]{4,1,3,2,0:T(2,128)} %copy.39), calls=%async_computation.1 | async-start | bytes 1048576 | tf_op jit(solution)/shard_map/all_to_all | solution.py:29
where the time goes:
time: 229 us; the launch traced here: 228 us
  blocking collectives  144 us (63%)
  waiting for transfers between devices  61.6 us (27%)
  local copies, waits for them, and re-layouts  10.5 us (5%)
  matrix products  5.55 us (2%)
  starting transfers between devices  5.48 us (2%)
    all_to_all x1, blocking collectives, on_device(): lax.all_to_all(blended, BAND, split_axis=1, concat_axis=2, tiled=True)  70.2 us
    all_to_all x1, waiting for transfers between devices, moved_by_axis(): lax.all_to_all(parts, axes[k], split_axis=k, concat_axis=k, tiled=True)  61.6 us
    all_to_all x1, blocking collectives, moved_by_axis(): lax.all_to_all(parts, axes[k], split_axis=k, concat_axis=k, tiled=True)  45.2 us
    all_to_all x1, blocking collectives, sent_to_all(): lax.all_to_all(jnp.broadcast_to(value[None], (size, *value.shape)), axis,...  28.8 us
    all_to_all x1, starting transfers between devices, moved_by_axis(): lax.all_to_all(parts, axes[k], split_axis=k, concat_axis=k, tiled=True)  5.48 us
  transfers between devices with their start and end apart: 1, of which 1 were waited for; matrix products, arithmetic and copies ran while one was open for 1% of the time, Pallas kernels for 0%

commit v1 on v0

v1 whole, which is shorter than its diff:
```python
import jax
import jax.numpy as jnp
from jax import lax
from jax.experimental import pallas as pl
from jax.experimental.pallas import tpu as pltpu
from jax.sharding import Mesh
from jax.sharding import PartitionSpec as P

BAND = ("band_0", "band_1")
GROUPS_BAND = ("groups", "band_0", "band_1")
EVERYONE = ("band_0", "band_1", "chan")
LANES = 128


def dot(a, b, dims):
    return lax.dot_general(
        a, b, (dims, ((), ())), precision=lax.Precision.HIGHEST, preferred_element_type=jnp.float32
    )


def lane_block(shape, width):
    return lax.broadcasted_iota(jnp.int32, shape, len(shape) - 1) // width


def blocks_transposed(parts):
    n = len(parts)
    width = LANES // n
    which = lane_block(parts[0].shape, width)
    out = []
    for b in range(n):
        total = None
        for a in range(n):
            shift = (width * (a - b)) % LANES
            moved = pltpu.roll(parts[a], shift, axis=1) if shift else parts[a]
            total = moved if total is None else jnp.where(which == a, moved, total)
        out.append(total)
    return out


def shifted_copies(taps_row, rows, size, first):
    wide = jnp.broadcast_to(taps_row, (rows, size))
    return pltpu.roll(wide, first % size, axis=1, stride=1, stride_axis=0)


def across_kernel(x_ref, taps_ref, out_ref, padded_ref, strip_ref):
    channels, rows, cols = x_ref.shape
    tiles = cols // LANES
    length = taps_ref.shape[1]
    padded_ref[...] = jnp.zeros(padded_ref.shape, jnp.float32)
    padded_ref[:, 0:length] = taps_ref[...]
    body = rows * tiles
    edge = jnp.zeros((rows, LANES), jnp.float32)
    filtered = []
    for c in range(channels):
        strip_ref[c, 0:rows, :] = edge
        strip_ref[c, body + rows : body + 2 * rows, :] = edge
        for t in range(tiles):
            strip_ref[c, rows * (t + 1) : rows * (t + 2), :] = x_ref[c, :, LANES * t : LANES * (t + 1)]
        table = shifted_copies(padded_ref[c : c + 1, :], LANES, padded_ref.shape[1], 0)
        total = None
        for k in range(3):
            part = dot(
                strip_ref[c, rows * k : rows * k + body, :],
                table[:, LANES * k : LANES * (k + 1)],
                ((1,), (1,)),
            )
            total = part if total is None else total + part
        filtered.append(total)
    packed = blocks_transposed(filtered)
    for q, value in enumerate(packed):
        for t in range(tiles):
            at = rows * (len(packed) * t + q)
            out_ref[at : at + rows, :] = value[rows * t : rows * (t + 1), :]


def tables_kernel(taps_ref, mix_ref, table_ref, wide_mix_ref, padded_ref):
    channels, length = taps_ref.shape
    size = table_ref.shape[1]
    margin = (length - 1) // 2
    padded_ref[...] = jnp.zeros(padded_ref.shape, jnp.float32)
    padded_ref[:, 0:length] = taps_ref[...]
    for c in range(channels):
        rolled = shifted_copies(padded_ref[c : c + 1, :], size, padded_ref.shape[1], -margin)
        table_ref[c] = rolled[:, 0:size]
    n = wide_mix_ref.shape[0]
    width = n // channels
    spread = (
        lax.broadcasted_iota(jnp.int32, (n, channels), 0) // width
        == lax.broadcasted_iota(jnp.int32, (n, channels), 1)
    ).astype(jnp.float32)
    tall = dot(spread, mix_ref[...], ((1,), (1,)))
    wide = dot(tall, spread, ((1,), (1,)))
    same = (
        lax.broadcasted_iota(jnp.int32, (n, n), 0) % width
        == lax.broadcasted_iota(jnp.int32, (n, n), 1) % width
    )
    wide_mix_ref[...] = jnp.where(same, wide, 0.0)


def vertical_kernel(in_ref, table_ref, wide_mix_ref, out_ref, gathered_ref, vertical_ref):
    height = gathered_ref.shape[1]
    quarters = gathered_ref.shape[0]
    sources = in_ref.shape[0] // (quarters * 4)
    rows = height // sources
    per = table_ref.shape[0] // quarters
    which = lane_block((height, LANES), LANES // per)
    for x in range(quarters):
        for s in range(sources):
            at = rows * (quarters * s + x)
            gathered_ref[x, rows * s : rows * (s + 1), :] = in_ref[at : at + rows, :]
        mine = gathered_ref[x]
        total = None
        for c in range(per):
            part = dot(table_ref[per * x + c], jnp.where(which == c, mine, 0.0), ((1,), (0,)))
            total = part if total is None else total + part
        vertical_ref[:, LANES * x : LANES * (x + 1)] = total
    mixed = dot(vertical_ref[...], wide_mix_ref[...], ((1,), (0,)))
    for x in range(quarters):
        for s in range(sources):
            at = rows * (quarters * s + x)
            out_ref[at : at + rows, :] = mixed[rows * s : rows * (s + 1), LANES * x : LANES * (x + 1)]


def unpack_kernel(in_ref, out_ref, strip_ref):
    channels, rows, cols = out_ref.shape
    tiles = cols // LANES
    quarters = strip_ref.shape[0]
    for q in range(quarters):
        for t in range(tiles):
            at = rows * (quarters * t + q)
            strip_ref[q, rows * t : rows * (t + 1), :] = in_ref[at : at + rows, :]
    joined = blocks_transposed([strip_ref[q] for q in range(quarters)])
    for o, value in enumerate(joined):
        for t in range(tiles):
            out_ref[o, :, LANES * t : LANES * (t + 1)] = value[rows * t : rows * (t + 1), :]


def on_device(slide_region, row_taps, column_taps, channel_mix):
    channels, rows, cols = slide_region.shape
    bands = lax.axis_size(BAND)
    quarters = lax.axis_size("chan")
    height = rows * bands
    everyone = bands * quarters
    all_channels = column_taps.shape[0]
    f32 = jnp.float32
    flat = jax.ShapeDtypeStruct((everyone * rows, LANES), f32)
    scratch = pltpu.VMEM

    packed = pl.pallas_call(
        across_kernel,
        out_shape=flat,
        scratch_shapes=[
            scratch((channels, 4 * LANES), f32),
            scratch((channels, rows * (cols // LANES + 2), LANES), f32),
        ],
        name="across",
    )(slide_region, row_taps)
    table, wide_mix = pl.pallas_call(
        tables_kernel,
        out_shape=(
            jax.ShapeDtypeStruct((all_channels, height, height), f32),
            jax.ShapeDtypeStruct((quarters * LANES, quarters * LANES), f32),
        ),
        scratch_shapes=[scratch((all_channels, 4 * LANES), f32)],
        name="tables",
    )(column_taps, channel_mix)

    def exchanged(value):
        parts = value.reshape(everyone, rows, LANES)
        return lax.all_to_all(parts, EVERYONE, 0, 0, tiled=True).reshape(value.shape)

    mixed = pl.pallas_call(
        vertical_kernel,
        out_shape=flat,
        scratch_shapes=[
            scratch((quarters, height, LANES), f32),
            scratch((height, quarters * LANES), f32),
        ],
        name="vertical",
    )(exchanged(packed), table, wide_mix)
    return pl.pallas_call(
        unpack_kernel,
        out_shape=jax.ShapeDtypeStruct((channels, rows, cols), f32),
        scratch_shapes=[scratch((quarters, rows * (cols // LANES), LANES), f32)],
        name="unpack",
    )(exchanged(mixed))


def solution(mesh):
    bands = mesh.shape["band"]
    split = Mesh(
        mesh.devices.reshape(mesh.shape["groups"], bands // 2, 2, mesh.shape["chan"]),
        ("groups", "band_0", "band_1", "chan"),
    )
    in_specs = (P("chan", GROUPS_BAND, None), P("chan", None), P(), P())
    out_specs = P("chan", GROUPS_BAND, None)
    return jax.shard_map(
        on_device, mesh=split, in_specs=in_specs, out_specs=out_specs, check_vma=False
    )
```

time: 229 us -> 206 us (0.90)
  blocking collectives: 144 us -> 75.1 us
  starting transfers between devices: 5.48 us -> 55.7 us
  Pallas kernels: 0 us -> 18.4 us
  local copies, waits for them, and re-layouts: 10.5 us -> 0.79 us
  waiting for transfers between devices: 61.6 us -> 55.2 us
  matrix products: 5.55 us -> 0 us
    all_to_all x3 -> x1, blocking collectives: 144 us -> 75.1 us  [exchanged(): lax.all_to_all(parts, EVERYONE, 0, 0, tiled=True).reshape(value.shape)]
    all_to_all x1, starting transfers between devices: 5.48 us -> 55.7 us  [exchanged(): lax.all_to_all(parts, EVERYONE, 0, 0, tiled=True).reshape(value.shape)]
    pallas_call x0 -> x4, Pallas kernels: none -> 18.4 us  [the longest x1 7.93 us: on_device(): pl.pallas_call(vertical_kernel, out_shape=flat, scratch_shapes=[scratch((...]
    all_to_all x1, waiting for transfers between devices: 61.6 us -> 55.2 us  [exchanged(): lax.all_to_all(parts, EVERYONE, 0, 0, tiled=True).reshape(value.shape)]
    dot_general x7 -> x0, matrix products: 5.55 us -> none  [the longest x1 1.8 us: on_device(): jnp.einsum('oc,chw->ohw', own_mixing, gathered_copies(vertical, 'chan', 0...]
    reshape x4 -> x0, local copies, waits for them, and re-layouts: 3.46 us -> none  [the longest x2 2 us: band_tables(): repeated.reshape(channels, tile_size, period - 1)[:, :, :3 * tile_size]]
    all_to_all x5 -> x0, local copies, waits for them, and re-layouts: 3 us -> none  [the longest x2 1.46 us: moved_by_axis(): lax.all_to_all(parts, axes[k], split_axis=k, concat_axis=k, tiled=True)]
  transfers between devices with their start and end apart: 1 -> 1, of which waited for: 1 -> 1; matrix products, arithmetic and copies ran while one was open for 1% -> 0% of each run, Pallas kernels for 0% -> 2%
where the time goes in v1:
time: 206 us; the launch traced here: 205 us
  blocking collectives  75.1 us (36%)
  starting transfers between devices  55.7 us (27%)
  waiting for transfers between devices  55.2 us (27%)
  Pallas kernels  18.4 us (9%)
    all_to_all x1, blocking collectives, exchanged(): lax.all_to_all(parts, EVERYONE, 0, 0, tiled=True).reshape(value.shape)  75.1 us
    all_to_all x1, starting transfers between devices, exchanged(): lax.all_to_all(parts, EVERYONE, 0, 0, tiled=True).reshape(value.shape)  55.7 us
    all_to_all x1, waiting for transfers between devices, exchanged(): lax.all_to_all(parts, EVERYONE, 0, 0, tiled=True).reshape(value.shape)  55.2 us
    pallas_call x1, Pallas kernels, on_device(): pl.pallas_call(vertical_kernel, out_shape=flat, scratch_shapes=[scratch((...  7.93 us
    pallas_call x1, Pallas kernels, on_device(): pl.pallas_call(tables_kernel, out_shape=(jax.ShapeDtypeStruct((all_channe...  4.45 us
  transfers between devices with their start and end apart: 1, of which 1 were waited for; matrix products, arithmetic and copies ran while one was open for 0% of the time, Pallas kernels for 2%

profile of v1, /device:TPU:33, one launch (start us, length us, event | category | flops | bytes accessed | tf_op | source)
XLA Modules:
  0.0 205.2 jit_solution(14506921255584311313)
XLA Ops:
  0.0 3.7 %across.1 = f32[1024,128]{1,0:T(8,128)} custom-call(f32[4,4,8192]{2,1,0:T(4,128)} %x_ref.1, f32[4,257]{1,0:T(4,128)} %taps_ref.2), custom_call_target="tpu_custom_call" | custom-call | tf_op jit(solution)/shard_map/across/pallas_call | solution.py:149
  3.7 55.7 %all-to-all-start = ((f32[256,4,128]{2,1,0:T(4,128)}), f32[256,4,128]{2,1,0:T(4,128)S(1)}, u32[]{:S(2)}, u32[]{:S(2)}) async-start(f32[256,4,128]{2,1,0:T(4,128)} %bitcast.6), calls=%async_computation | async-start | bytes 1048576 | tf_op jit(solution)/shard_map/all_to_all | solution.py:170
  59.4 4.4 %tables.1 = (f32[16,256,256]{2,1,0:T(8,128)}, f32[512,512]{1,0:T(8,128)}) custom-call(f32[16,257]{1,0:T(8,128)} %taps_ref.3, f32[16,16]{1,0:T(8,128)} %mix_ref.1), custom_call_target="tpu_custom_call" | custom-call | tf_op jit(solution)/shard_map/tables/pallas_call | solution.py:158
  63.8 55.2 %all-to-all-done = f32[256,4,128]{2,1,0:T(4,128)S(1)} async-done(((f32[256,4,128]{2,1,0:T(4,128)}), f32[256,4,128]{2,1,0:T(4,128)S(1)}, u32[]{:S(2)}, u32[]{:S(2)}) %all-to-all-start) | async-done | bytes 524320 | tf_op jit(solution)/shard_map/all_to_all | solution.py:170
  119.1 0.0 copy-start
  119.1 0.8 copy-done
  119.9 7.9 %vertical.1 = f32[1024,128]{1,0:T(8,128)} custom-call(f32[1024,128]{1,0:T(8,128)} %bitcast.4, f32[16,256,256]{2,1,0:T(8,128)} %get-tuple-element.7.table_ref, f32[512,512]{1,0:T(8,128)} %get-tuple-element.8.wide_mix_ref), custom_call_target="tpu_custom_call" | custom-call | tf_op jit(solution)/shard_map/vertical/pallas_call | solution.py:172
  127.8 75.1 %all_to_all.10 = f32[256,4,128]{2,1,0:T(4,128)} all-to-all(f32[256,4,128]{2,1,0:T(4,128)} %bitcast.5), channel_id=1, replica_groups=mesh['groups'=2,'band_0'=32,'band_1'=2,'chan'=4] {'band_0','band_1','chan'}, dimensions={0} | all-to-all | bytes 1048576 | tf_op jit(solution)/shard_map/all_to_all | solution.py:170
  202.8 2.3 %unpack.1 = f32[4,4,8192]{2,1,0:T(4,128)} custom-call(f32[1024,128]{1,0:T(8,128)} %bitcast.7), custom_call_target="tpu_custom_call" | custom-call | tf_op jit(solution)/shard_map/unpack/pallas_call | solution.py:181
Async XLA Ops:
  3.7 115.4 %all-to-all-start = ((f32[256,4,128]{2,1,0:T(4,128)}), f32[256,4,128]{2,1,0:T(4,128)S(1)}, u32[]{:S(2)}, u32[]{:S(2)}) async-start(f32[256,4,128]{2,1,0:T(4,128)} %bitcast.6), calls=%async_computation | async-start | bytes 1048576 | tf_op jit(solution)/shard_map/all_to_all | solution.py:170
  119.1 0.8 copy-start

commit v2 on v1

v2 whole, which is shorter than its diff:
```python
import jax
import jax.numpy as jnp
from jax import lax
from jax.experimental import pallas as pl
from jax.experimental.pallas import tpu as pltpu
from jax.sharding import Mesh
from jax.sharding import PartitionSpec as P

BAND = ("band_0", "band_1")
GROUPS_BAND = ("groups", "band_0", "band_1")
EVERYONE = ("band_0", "band_1", "chan")
LANES = 128
F32 = jnp.float32
BF16 = jnp.bfloat16
IN_VMEM = pl.BlockSpec(memory_space=pltpu.VMEM)
IN_HBM = pl.BlockSpec(memory_space=pltpu.HBM)
SMALL = pltpu.CompilerParams(vmem_limit_bytes=16 * 1024 * 1024)


def halves(value):
    high = value.astype(BF16)
    return high, (value - high.astype(F32)).astype(BF16)


def dot(a, b, dims):
    return lax.dot_general(a, b, (dims, ((), ())), preferred_element_type=F32)


def dot_of_halves(a, b, dims):
    (a_high, a_low), (b_high, b_low) = a, b
    return dot(a_high, b_high, dims) + (dot(a_high, b_low, dims) + dot(a_low, b_high, dims))


def lane_block(shape, width):
    return lax.broadcasted_iota(jnp.int32, shape, len(shape) - 1) // width


def blocks_transposed(parts, wanted):
    width = LANES // len(parts)
    which = lane_block(parts[0].shape, width)
    out = []
    for b in wanted:
        total = None
        for a, part in enumerate(parts):
            shift = (width * (a - b)) % LANES
            moved = pltpu.roll(part, shift, axis=1) if shift else part
            total = moved if total is None else jnp.where(which == a, moved, total)
        out.append(total)
    return out


def shifted_copies(taps_row, rows, size, first):
    wide = jnp.broadcast_to(taps_row, (rows, size))
    return pltpu.roll(wide, first % size, axis=1, stride=1, stride_axis=0)


def across_kernel(x_hbm, taps_ref, out_ref, x_ref, padded_ref, lhs_ref, arrived):
    channels, rows, cols = x_ref.shape
    tiles = cols // LANES
    pairs = tiles // 2
    body = rows * pairs
    length = taps_ref.shape[1]
    copies = [pltpu.make_async_copy(x_hbm.at[c], x_ref.at[c], arrived.at[c]) for c in range(channels)]
    for copy in copies:
        copy.start()
    padded_ref[...] = jnp.zeros(padded_ref.shape, F32)
    padded_ref[:, 0:length] = taps_ref[...]
    edge = jnp.zeros((rows, LANES), F32)
    filtered = ([], [])
    for c in range(channels):
        table = halves(shifted_copies(padded_ref[c : c + 1, :], 2 * LANES, padded_ref.shape[1], 0))
        lhs_ref[c, 0:rows, 0:LANES] = edge
        lhs_ref[c, body - rows : body, 3 * LANES : 4 * LANES] = edge
        copies[c].wait()
        for t in range(tiles):
            tile = x_ref[c, :, LANES * t : LANES * (t + 1)]
            p, odd = t // 2, t % 2
            lhs_ref[c, rows * p : rows * (p + 1), LANES * (1 + odd) : LANES * (2 + odd)] = tile
            q = p + 1 if odd else p - 1
            if 0 <= q < pairs:
                at = 0 if odd else 3 * LANES
                lhs_ref[c, rows * q : rows * (q + 1), at : at + LANES] = tile
        total = dot_of_halves(halves(lhs_ref[c]), table, ((1,), (1,)))
        filtered[0].append(total[:, 0:LANES])
        filtered[1].append(total[:, LANES : 2 * LANES])
    for odd in range(2):
        packed = blocks_transposed(filtered[odd], range(channels))
        for q, value in enumerate(packed):
            for p in range(pairs):
                at = rows * (channels * (2 * p + odd) + q)
                out_ref[at : at + rows, :] = value[rows * p : rows * (p + 1), :]


def tables_kernel(taps_ref, mix_ref, high_ref, low_ref, wide_mix_ref, padded_ref):
    channels, length = taps_ref.shape
    quarters, half = high_ref.shape[0:2]
    margin = (length - 1) // 2
    padded_ref[...] = jnp.zeros(padded_ref.shape, F32)
    padded_ref[:, 0:length] = taps_ref[...]
    per = channels // quarters
    for c in range(channels):
        rolled = shifted_copies(padded_ref[c : c + 1, :], half, padded_ref.shape[1], half - margin)
        high, low = halves(rolled[:, 0 : 3 * half])
        at = 3 * half * (c % per)
        high_ref[c // per, :, at : at + 3 * half] = high
        low_ref[c // per, :, at : at + 3 * half] = low
    n = wide_mix_ref.shape[1]
    width = n // channels
    spread = (
        lax.broadcasted_iota(jnp.int32, (n, channels), 0) // width
        == lax.broadcasted_iota(jnp.int32, (n, channels), 1)
    ).astype(F32)
    precise = dict(precision=lax.Precision.HIGHEST, preferred_element_type=F32)
    tall = lax.dot_general(spread, mix_ref[...], (((1,), (1,)), ((), ())), **precise)
    wide = lax.dot_general(tall, spread, (((1,), (1,)), ((), ())), **precise)
    same = (
        lax.broadcasted_iota(jnp.int32, (n, n), 0) % width
        == lax.broadcasted_iota(jnp.int32, (n, n), 1) % width
    )
    wide_mix_ref[0], wide_mix_ref[1] = halves(jnp.where(same, wide, 0.0))


def vertical_kernel(
    strip, in_ref, high_ref, low_hbm, mix_hbm, out_ref, gathered_ref, vertical_ref, low_ref, mix_ref, arrived
):
    quarters, height = gathered_ref.shape[0:2]
    half = height // 2
    per = high_ref.shape[2] // (3 * half)
    sources = height // strip
    low_copy = pltpu.make_async_copy(low_hbm, low_ref, arrived.at[0])
    mix_copy = pltpu.make_async_copy(mix_hbm, mix_ref, arrived.at[1])
    low_copy.start()
    mix_copy.start()
    which = lane_block((height, LANES), LANES // per)
    masked = []
    for x in range(quarters):
        for s in range(sources):
            at = strip * (quarters * s + x)
            gathered_ref[x, strip * s : strip * (s + 1), :] = in_ref[at : at + strip, :]
        mine = gathered_ref[x]
        masked.append([halves(jnp.where(which == c, mine, 0.0)) for c in range(per)])

    def filtered(table_ref, x, parts):
        for h in range(2):
            total = None
            for c in range(per):
                at = half * (3 * c + 1 - h)
                rows = table_ref[x, :, at : at + height]
                for k in parts:
                    part = dot(rows, masked[x][c][k], ((1,), (0,)))
                    total = part if total is None else total + part
            yield slice(half * h, half * (h + 1)), slice(LANES * x, LANES * (x + 1)), total

    for x in range(quarters):
        for at, lanes, total in filtered(high_ref, x, (0, 1)):
            vertical_ref[at, lanes] = total
    low_copy.wait()
    for x in range(quarters):
        for at, lanes, total in filtered(low_ref, x, (0,)):
            vertical_ref[at, lanes] += total
    mix_copy.wait()
    mixed = dot_of_halves(halves(vertical_ref[...]), (mix_ref[0], mix_ref[1]), ((1,), (0,)))
    for x in range(quarters):
        for s in range(sources):
            at = strip * (quarters * s + x)
            out_ref[at : at + strip, :] = mixed[strip * s : strip * (s + 1), LANES * x : LANES * (x + 1)]


def unpack_kernel(in_ref, out_hbm, out_ref, strip_ref, sent):
    channels, rows, cols = out_ref.shape
    tiles = cols // LANES
    quarters = strip_ref.shape[0]
    for q in range(quarters):
        for t in range(tiles):
            at = rows * (quarters * t + q)
            strip_ref[q, rows * t : rows * (t + 1), :] = in_ref[at : at + rows, :]
    parts = [strip_ref[q] for q in range(quarters)]
    copies = [pltpu.make_async_copy(out_ref.at[o], out_hbm.at[o], sent.at[o]) for o in range(channels)]
    for o in range(channels):
        (value,) = blocks_transposed(parts, [o])
        for t in range(tiles):
            out_ref[o, :, LANES * t : LANES * (t + 1)] = value[rows * t : rows * (t + 1), :]
        copies[o].start()
    for copy in copies:
        copy.wait()


def in_vmem(value):
    return pltpu.with_memory_space_constraint(value, pltpu.VMEM)


def in_hbm(value):
    return pltpu.with_memory_space_constraint(value, pltpu.HBM)


def on_device(slide_region, row_taps, column_taps, channel_mix):
    channels, rows, cols = slide_region.shape
    bands = lax.axis_size(BAND)
    quarters = lax.axis_size("chan")
    height = rows * bands
    everyone = bands * quarters
    all_channels = column_taps.shape[0]
    per = all_channels // quarters
    flat = pltpu.VMEM((everyone * rows, LANES), F32)
    scratch = pltpu.VMEM
    lanes = quarters * LANES

    packed = pl.pallas_call(
        across_kernel,
        out_shape=flat,
        in_specs=[IN_HBM, pl.BlockSpec()],
        out_specs=IN_VMEM,
        scratch_shapes=[
            scratch((channels, rows, cols), F32),
            scratch((channels, 4 * LANES), F32),
            scratch((channels, rows * (cols // (2 * LANES)), 4 * LANES), F32),
            pltpu.SemaphoreType.DMA((channels,)),
        ],
        compiler_params=SMALL,
        name="across",
    )(in_hbm(slide_region), in_hbm(row_taps))
    table = (quarters, height // 2, per * (height // 2) * 3)
    high, low, wide_mix = pl.pallas_call(
        tables_kernel,
        out_shape=(
            pltpu.VMEM(table, BF16),
            pltpu.HBM(table, BF16),
            pltpu.HBM((2, lanes, lanes), BF16),
        ),
        in_specs=[pl.BlockSpec(), pl.BlockSpec()],
        out_specs=[IN_VMEM, pl.BlockSpec(), pl.BlockSpec()],
        scratch_shapes=[scratch((all_channels, 4 * LANES), F32)],
        compiler_params=SMALL,
        name="tables",
    )(in_hbm(column_taps), in_hbm(channel_mix))

    def exchanged(value):
        parts = value.reshape(everyone, rows, LANES)
        moved = lax.all_to_all(parts, EVERYONE, 0, 0, tiled=True)
        return in_vmem(moved.reshape(value.shape))

    mixed = pl.pallas_call(
        lambda *refs: vertical_kernel(rows, *refs),
        out_shape=flat,
        in_specs=[IN_VMEM, IN_VMEM, IN_HBM, IN_HBM],
        out_specs=IN_VMEM,
        scratch_shapes=[
            scratch((quarters, height, LANES), F32),
            scratch((height, lanes), F32),
            scratch(table, BF16),
            scratch((2, lanes, lanes), BF16),
            pltpu.SemaphoreType.DMA((2,)),
        ],
        compiler_params=SMALL,
        name="vertical",
    )(exchanged(packed), in_vmem(high), in_hbm(low), in_hbm(wide_mix))
    return pl.pallas_call(
        unpack_kernel,
        out_shape=jax.ShapeDtypeStruct((channels, rows, cols), F32),
        in_specs=[IN_VMEM],
        out_specs=IN_HBM,
        scratch_shapes=[
            scratch((channels, rows, cols), F32),
            scratch((quarters, rows * (cols // LANES), LANES), F32),
            pltpu.SemaphoreType.DMA((channels,)),
        ],
        compiler_params=SMALL,
        name="unpack",
    )(exchanged(mixed))


def solution(mesh):
    bands = mesh.shape["band"]
    split = Mesh(
        mesh.devices.reshape(mesh.shape["groups"], bands // 2, 2, mesh.shape["chan"]),
        ("groups", "band_0", "band_1", "chan"),
    )
    in_specs = (P("chan", GROUPS_BAND, None), P("chan", None), P(), P())
    out_specs = P("chan", GROUPS_BAND, None)
    return jax.shard_map(
        on_device, mesh=split, in_specs=in_specs, out_specs=out_specs, check_vma=False
    )
```

time: 206 us -> 201 us (0.976)
  Pallas kernels: 18.4 us -> 13.7 us
    pallas_call x3, Pallas kernels: 16.1 us -> 12.5 us  [the longest x1 4.86 us: on_device(): pl.pallas_call(across_kernel, out_shape=flat, in_specs=[IN_HBM, pl.BlockS...]
where the time goes in v2:
time: 201 us; the launch traced here: 200 us
  blocking collectives  74.7 us (37%)
  waiting for transfers between devices  55.9 us (28%)
  starting transfers between devices  55.7 us (28%)
  Pallas kernels  13.7 us (7%)
    all_to_all x1, blocking collectives, exchanged(): moved = lax.all_to_all(parts, EVERYONE, 0, 0, tiled=True)  74.7 us
    all_to_all x1, waiting for transfers between devices, exchanged(): moved = lax.all_to_all(parts, EVERYONE, 0, 0, tiled=True)  55.9 us
    all_to_all x1, starting transfers between devices, exchanged(): moved = lax.all_to_all(parts, EVERYONE, 0, 0, tiled=True)  55.7 us
    pallas_call x1, Pallas kernels, on_device(): pl.pallas_call(across_kernel, out_shape=flat, in_specs=[IN_HBM, pl.BlockS...  4.86 us
  transfers between devices with their start and end apart: 1, of which 1 were waited for; matrix products, arithmetic and copies ran while one was open for 0% of the time, Pallas kernels for 2%

profile of v2, /device:TPU:33, one launch (start us, length us, event | category | flops | bytes accessed | tf_op | source)
XLA Modules:
  0.0 200.3 jit_solution(14505963566509545463)
XLA Ops:
  0.0 4.9 %across.1 = f32[1024,128]{1,0:T(8,128)} custom-call(f32[4,4,8192]{2,1,0:T(4,128)} %x_hbm.1, f32[4,257]{1,0:T(4,128)} %taps_ref.2), custom_call_target="tpu_custom_call" | custom-call | tf_op jit(solution)/shard_map/across/pallas_call | solution.py:208
  4.9 55.7 %all-to-all-start = ((f32[256,4,128]{2,1,0:T(4,128)}), f32[256,4,128]{2,1,0:T(4,128)S(1)}, u32[]{:S(2)}, u32[]{:S(2)}) async-start(f32[256,4,128]{2,1,0:T(4,128)} %bitcast), calls=%async_computation | async-start | bytes 1048576 | tf_op jit(solution)/shard_map/all_to_all | solution.py:239
  60.6 3.8 %tables.1 = (bf16[4,128,1536]{2,1,0:T(8,128)(2,1)S(1)}, bf16[4,128,1536]{2,1,0:T(8,128)(2,1)}, bf16[2,512,512]{2,1,0:T(8,128)(2,1)}) custom-call(f32[16,257]{1,0:T(8,128)} %taps_ref.3, f32[16,16]{1,0:T(8,128)} %mix_ref.1), custom_call_target="tpu_custom_call" | custom-call | tf_op jit(solution)/shard_map/tables/pallas_call | solution.py:223
  64.4 55.9 %all-to-all-done = f32[256,4,128]{2,1,0:T(4,128)S(1)} async-done(((f32[256,4,128]{2,1,0:T(4,128)}), f32[256,4,128]{2,1,0:T(4,128)S(1)}, u32[]{:S(2)}, u32[]{:S(2)}) %all-to-all-start) | async-done | bytes 524320 | tf_op jit(solution)/shard_map/all_to_all | solution.py:239
  120.3 3.9 %vertical.1 = f32[1024,128]{1,0:T(8,128)S(1)} custom-call(f32[1024,128]{1,0:T(8,128)S(1)} %bitcast.4, bf16[4,128,1536]{2,1,0:T(8,128)(2,1)S(1)} %get-tuple-element.8.refs_1_, bf16[4,128,1536]{2,1,0:T(8,128)(2,1)} %get-tuple-element.9.refs_2_, bf16[2,512,512]{2,1,0:T(8,128)(2,1)} %get-tuple-element.10.refs_3_), custom_call_target="tpu_custom_call" | custom-call | tf_op jit(solution)/shard_map/vertical/pallas_call | solution.py:242
  124.1 74.7 %all_to_all.10 = f32[256,4,128]{2,1,0:T(4,128)S(1)} all-to-all(f32[256,4,128]{2,1,0:T(4,128)S(1)} %bitcast.5), channel_id=1, replica_groups=mesh['groups'=2,'band_0'=32,'band_1'=2,'chan'=4] {'band_0','band_1','chan'}, dimensions={0} | all-to-all | bytes 1048576 | tf_op jit(solution)/shard_map/all_to_all | solution.py:239
  198.9 1.2 unpack.1
Async XLA Ops:
  4.9 115.4 %all-to-all-start = ((f32[256,4,128]{2,1,0:T(4,128)}), f32[256,4,128]{2,1,0:T(4,128)S(1)}, u32[]{:S(2)}, u32[]{:S(2)}) async-start(f32[256,4,128]{2,1,0:T(4,128)} %bitcast), calls=%async_computation | async-start | bytes 1048576 | tf_op jit(solution)/shard_map/all_to_all | solution.py:239

commit v3 on v2

--- a/solution.py
+++ b/solution.py
@@ -10,6 +10,7 @@
 GROUPS_BAND = ("groups", "band_0", "band_1")
 EVERYONE = ("band_0", "band_1", "chan")
 LANES = 128
+SUBLANES = 8
 F32 = jnp.float32
 BF16 = jnp.bfloat16
 IN_VMEM = pl.BlockSpec(memory_space=pltpu.VMEM)
@@ -54,41 +55,33 @@
     return pltpu.roll(wide, first % size, axis=1, stride=1, stride_axis=0)
 
 
-def across_kernel(x_hbm, taps_ref, out_ref, x_ref, padded_ref, lhs_ref, arrived):
-    channels, rows, cols = x_ref.shape
-    tiles = cols // LANES
-    pairs = tiles // 2
-    body = rows * pairs
+def across_kernel(rows, x_hbm, taps_ref, out_ref, x_ref, padded_ref, arrived):
+    channels, body = x_hbm.shape[0:2]
     length = taps_ref.shape[1]
-    copies = [pltpu.make_async_copy(x_hbm.at[c], x_ref.at[c], arrived.at[c]) for c in range(channels)]
+    copies = [
+        pltpu.make_async_copy(x_hbm.at[c], x_ref.at[c, pl.ds(SUBLANES, body), :], arrived.at[c])
+        for c in range(channels)
+    ]
     for copy in copies:
         copy.start()
     padded_ref[...] = jnp.zeros(padded_ref.shape, F32)
     padded_ref[:, 0:length] = taps_ref[...]
-    edge = jnp.zeros((rows, LANES), F32)
-    filtered = ([], [])
+    edge = jnp.zeros((SUBLANES, LANES), F32)
+    filtered = []
     for c in range(channels):
-        table = halves(shifted_copies(padded_ref[c : c + 1, :], 2 * LANES, padded_ref.shape[1], 0))
-        lhs_ref[c, 0:rows, 0:LANES] = edge
-        lhs_ref[c, body - rows : body, 3 * LANES : 4 * LANES] = edge
+        x_ref[c, 0:SUBLANES, :] = edge
+        x_ref[c, SUBLANES + body : 2 * SUBLANES + body, :] = edge
+        rolled = shifted_copies(padded_ref[c : c + 1, :], LANES, padded_ref.shape[1], 0)
+        table = halves(rolled[:, 0 : 3 * LANES])
         copies[c].wait()
-        for t in range(tiles):
-            tile = x_ref[c, :, LANES * t : LANES * (t + 1)]
-            p, odd = t // 2, t % 2
-            lhs_ref[c, rows * p : rows * (p + 1), LANES * (1 + odd) : LANES * (2 + odd)] = tile
-            q = p + 1 if odd else p - 1
-            if 0 <= q < pairs:
-                at = 0 if odd else 3 * LANES
-                lhs_ref[c, rows * q : rows * (q + 1), at : at + LANES] = tile
-        total = dot_of_halves(halves(lhs_ref[c]), table, ((1,), (1,)))
-        filtered[0].append(total[:, 0:LANES])
-        filtered[1].append(total[:, LANES : 2 * LANES])
-    for odd in range(2):
-        packed = blocks_transposed(filtered[odd], range(channels))
-        for q, value in enumerate(packed):
-            for p in range(pairs):
-                at = rows * (channels * (2 * p + odd) + q)
-                out_ref[at : at + rows, :] = value[rows * p : rows * (p + 1), :]
+        first = SUBLANES - rows
+        near = [x_ref[c, first + rows * k : first + rows * k + body, :] for k in range(3)]
+        filtered.append(dot_of_halves(halves(jnp.concatenate(near, axis=1)), table, ((1,), (1,))))
+    packed = blocks_transposed(filtered, range(channels))
+    for q, value in enumerate(packed):
+        for t in range(body // rows):
+            at = rows * (channels * t + q)
+            out_ref[at : at + rows, :] = value[rows * t : rows * (t + 1), :]
 
 
 def tables_kernel(taps_ref, mix_ref, high_ref, low_ref, wide_mix_ref, padded_ref):
@@ -121,16 +114,14 @@
 
 
 def vertical_kernel(
-    strip, in_ref, high_ref, low_hbm, mix_hbm, out_ref, gathered_ref, vertical_ref, low_ref, mix_ref, arrived
+    strip, in_ref, high_ref, low_hbm, mix_ref, out_ref, gathered_ref, vertical_ref, low_ref, arrived
 ):
     quarters, height = gathered_ref.shape[0:2]
     half = height // 2
     per = high_ref.shape[2] // (3 * half)
     sources = height // strip
-    low_copy = pltpu.make_async_copy(low_hbm, low_ref, arrived.at[0])
-    mix_copy = pltpu.make_async_copy(mix_hbm, mix_ref, arrived.at[1])
+    low_copy = pltpu.make_async_copy(low_hbm, low_ref, arrived)
     low_copy.start()
-    mix_copy.start()
     which = lane_block((height, LANES), LANES // per)
     masked = []
     for x in range(quarters):
@@ -154,32 +145,29 @@
     for x in range(quarters):
         for at, lanes, total in filtered(high_ref, x, (0, 1)):
             vertical_ref[at, lanes] = total
+    mixed = dot_of_halves(halves(vertical_ref[...]), (mix_ref[0], mix_ref[1]), ((1,), (0,)))
     low_copy.wait()
     for x in range(quarters):
         for at, lanes, total in filtered(low_ref, x, (0,)):
-            vertical_ref[at, lanes] += total
-    mix_copy.wait()
-    mixed = dot_of_halves(halves(vertical_ref[...]), (mix_ref[0], mix_ref[1]), ((1,), (0,)))
+            vertical_ref[at, lanes] = total
+    mixed = mixed + dot(vertical_ref[...].astype(BF16), mix_ref[0], ((1,), (0,)))
     for x in range(quarters):
         for s in range(sources):
             at = strip * (quarters * s + x)
             out_ref[at : at + strip, :] = mixed[strip * s : strip * (s + 1), LANES * x : LANES * (x + 1)]
 
 
-def unpack_kernel(in_ref, out_hbm, out_ref, strip_ref, sent):
-    channels, rows, cols = out_ref.shape
-    tiles = cols // LANES
+def unpack_kernel(rows, in_ref, out_hbm, out_ref, strip_ref, sent):
+    channels, body = out_ref.shape[0:2]
     quarters = strip_ref.shape[0]
     for q in range(quarters):
-        for t in range(tiles):
+        for t in range(body // rows):
             at = rows * (quarters * t + q)
             strip_ref[q, rows * t : rows * (t + 1), :] = in_ref[at : at + rows, :]
     parts = [strip_ref[q] for q in range(quarters)]
     copies = [pltpu.make_async_copy(out_ref.at[o], out_hbm.at[o], sent.at[o]) for o in range(channels)]
     for o in range(channels):
-        (value,) = blocks_transposed(parts, [o])
-        for t in range(tiles):
-            out_ref[o, :, LANES * t : LANES * (t + 1)] = value[rows * t : rows * (t + 1), :]
+        (out_ref[o],) = blocks_transposed(parts, [o])
         copies[o].start()
     for copy in copies:
         copy.wait()
@@ -205,30 +193,32 @@
     scratch = pltpu.VMEM
     lanes = quarters * LANES
 
+    tiles = cols // LANES
+    stacked = (channels, tiles * rows, LANES)
+    by_tile = slide_region.reshape(channels, rows, tiles, LANES).transpose(0, 2, 1, 3).reshape(stacked)
     packed = pl.pallas_call(
-        across_kernel,
+        lambda *refs: across_kernel(rows, *refs),
         out_shape=flat,
         in_specs=[IN_HBM, pl.BlockSpec()],
         out_specs=IN_VMEM,
         scratch_shapes=[
-            scratch((channels, rows, cols), F32),
+            scratch((channels, tiles * rows + 2 * SUBLANES, LANES), F32),
             scratch((channels, 4 * LANES), F32),
-            scratch((channels, rows * (cols // (2 * LANES)), 4 * LANES), F32),
             pltpu.SemaphoreType.DMA((channels,)),
         ],
         compiler_params=SMALL,
         name="across",
-    )(in_hbm(slide_region), in_hbm(row_taps))
+    )(in_hbm(by_tile), in_hbm(row_taps))
     table = (quarters, height // 2, per * (height // 2) * 3)
     high, low, wide_mix = pl.pallas_call(
         tables_kernel,
         out_shape=(
             pltpu.VMEM(table, BF16),
             pltpu.HBM(table, BF16),
-            pltpu.HBM((2, lanes, lanes), BF16),
+            pltpu.VMEM((2, lanes, lanes), BF16),
         ),
         in_specs=[pl.BlockSpec(), pl.BlockSpec()],
-        out_specs=[IN_VMEM, pl.BlockSpec(), pl.BlockSpec()],
+        out_specs=[IN_VMEM, pl.BlockSpec(), IN_VMEM],
         scratch_shapes=[scratch((all_channels, 4 * LANES), F32)],
         compiler_params=SMALL,
         name="tables",
@@ -242,31 +232,31 @@
     mixed = pl.pallas_call(
         lambda *refs: vertical_kernel(rows, *refs),
         out_shape=flat,
-        in_specs=[IN_VMEM, IN_VMEM, IN_HBM, IN_HBM],
+        in_specs=[IN_VMEM, IN_VMEM, IN_HBM, IN_VMEM],
         out_specs=IN_VMEM,
         scratch_shapes=[
             scratch((quarters, height, LANES), F32),
             scratch((height, lanes), F32),
             scratch(table, BF16),
-            scratch((2, lanes, lanes), BF16),
-            pltpu.SemaphoreType.DMA((2,)),
+            pltpu.SemaphoreType.DMA,
         ],
         compiler_params=SMALL,
         name="vertical",
-    )(exchanged(packed), in_vmem(high), in_hbm(low), in_hbm(wide_mix))
-    return pl.pallas_call(
-        unpack_kernel,
-        out_shape=jax.ShapeDtypeStruct((channels, rows, cols), F32),
+    )(exchanged(packed), in_vmem(high), in_hbm(low), in_vmem(wide_mix))
+    joined = pl.pallas_call(
+        lambda *refs: unpack_kernel(rows, *refs),
+        out_shape=pltpu.HBM(stacked, F32),
         in_specs=[IN_VMEM],
         out_specs=IN_HBM,
         scratch_shapes=[
-            scratch((channels, rows, cols), F32),
-            scratch((quarters, rows * (cols // LANES), LANES), F32),
+            scratch(stacked, F32),
+            scratch((quarters, tiles * rows, LANES), F32),
             pltpu.SemaphoreType.DMA((channels,)),
         ],
         compiler_params=SMALL,
         name="unpack",
     )(exchanged(mixed))
+    return joined.reshape(channels, tiles, rows, LANES).transpose(0, 2, 1, 3).reshape(channels, rows, cols)
 
 
 def solution(mesh):

time: 201 us -> 198 us (0.985)
  Pallas kernels: 13.7 us -> 11.1 us
where the time goes in v3:
time: 198 us
  blocking collectives  74.8 us (38%)
  waiting for transfers between devices  56.2 us (28%)
  starting transfers between devices  55.7 us (28%)
  Pallas kernels  11.1 us (6%)
    all_to_all x1, blocking collectives, exchanged(): moved = lax.all_to_all(parts, EVERYONE, 0, 0, tiled=True)  74.8 us
    all_to_all x1, waiting for transfers between devices, exchanged(): moved = lax.all_to_all(parts, EVERYONE, 0, 0, tiled=True)  56.2 us
    all_to_all x1, starting transfers between devices, exchanged(): moved = lax.all_to_all(parts, EVERYONE, 0, 0, tiled=True)  55.7 us
    pallas_call x1, Pallas kernels, on_device(): pl.pallas_call(lambda *refs: across_kernel(rows, *refs), out_shape=flat,...  4 us
  transfers between devices with their start and end apart: 1, of which 1 were waited for; matrix products, arithmetic and copies ran while one was open for 0% of the time, Pallas kernels for 2%

profile of v3, /device:TPU:33, one launch (start us, length us, event | category | flops | bytes accessed | tf_op | source)
XLA Modules:
  0.0 197.9 jit_solution(2997287885737027653)
XLA Ops:
  0.0 4.0 %across.1 = f32[1024,128]{1,0:T(8,128)} custom-call(f32[4,256,128]{2,1,0:T(8,128)} %bitcast.17, f32[4,257]{1,0:T(4,128)} %refs_1_.1), custom_call_target="tpu_custom_call" | custom-call | tf_op jit(solution)/shard_map/across/pallas_call | solution.py:199
  4.0 55.7 %all-to-all-start = ((f32[256,4,128]{2,1,0:T(4,128)}), f32[256,4,128]{2,1,0:T(4,128)S(1)}, u32[]{:S(2)}, u32[]{:S(2)}) async-start(f32[256,4,128]{2,1,0:T(4,128)} %bitcast.3), calls=%async_computation | async-start | bytes 1048576 | tf_op jit(solution)/shard_map/all_to_all | solution.py:229
  59.7 3.5 %tables.1 = (bf16[4,128,1536]{2,1,0:T(8,128)(2,1)S(1)}, bf16[4,128,1536]{2,1,0:T(8,128)(2,1)}, bf16[2,512,512]{2,1,0:T(8,128)(2,1)S(1)}) custom-call(f32[16,257]{1,0:T(8,128)} %taps_ref.1, f32[16,16]{1,0:T(8,128)} %mix_ref.1), custom_call_target="tpu_custom_call" | custom-call | tf_op jit(solution)/shard_map/tables/pallas_call | solution.py:213
  63.2 56.2 %all-to-all-done = f32[256,4,128]{2,1,0:T(4,128)S(1)} async-done(((f32[256,4,128]{2,1,0:T(4,128)}), f32[256,4,128]{2,1,0:T(4,128)S(1)}, u32[]{:S(2)}, u32[]{:S(2)}) %all-to-all-start) | async-done | bytes 524320 | tf_op jit(solution)/shard_map/all_to_all | solution.py:229
  119.4 2.4 %vertical.1 = f32[1024,128]{1,0:T(8,128)S(1)} custom-call(f32[1024,128]{1,0:T(8,128)S(1)} %bitcast.14, bf16[4,128,1536]{2,1,0:T(8,128)(2,1)S(1)} %get-tuple-element.8.refs_1_, bf16[4,128,1536]{2,1,0:T(8,128)(2,1)} %get-tuple-element.9.refs_2_, bf16[2,512,512]{2,1,0:T(8,128)(2,1)S(1)} %get-tuple-element.10.refs_3_), custom_call_target="tpu_custom_call" | custom-call | tf_op jit(solution)/shard_map/vertical/pallas_call | solution.py:232
  121.8 74.8 %all_to_all.10 = f32[256,4,128]{2,1,0:T(4,128)S(1)} all-to-all(f32[256,4,128]{2,1,0:T(4,128)S(1)} %bitcast.15), channel_id=1, replica_groups=mesh['groups'=2,'band_0'=32,'band_1'=2,'chan'=4] {'band_0','band_1','chan'}, dimensions={0} | all-to-all | bytes 1048576 | tf_op jit(solution)/shard_map/all_to_all | solution.py:229
  196.6 1.2 unpack.1
Async XLA Ops:
  4.0 115.4 %all-to-all-start = ((f32[256,4,128]{2,1,0:T(4,128)}), f32[256,4,128]{2,1,0:T(4,128)S(1)}, u32[]{:S(2)}, u32[]{:S(2)}) async-start(f32[256,4,128]{2,1,0:T(4,128)} %bitcast.3), calls=%async_computation | async-start | bytes 1048576 | tf_op jit(solution)/shard_map/all_to_all | solution.py:229

commit v4 on v3

--- a/solution.py
+++ b/solution.py
@@ -11,6 +11,7 @@
 EVERYONE = ("band_0", "band_1", "chan")
 LANES = 128
 SUBLANES = 8
+PARTS = 1
 F32 = jnp.float32
 BF16 = jnp.bfloat16
 IN_VMEM = pl.BlockSpec(memory_space=pltpu.VMEM)
@@ -55,33 +56,49 @@
     return pltpu.roll(wide, first % size, axis=1, stride=1, stride_axis=0)
 
 
-def across_kernel(rows, x_hbm, taps_ref, out_ref, x_ref, padded_ref, arrived):
+def across_kernel(rows, x_hbm, taps_ref, out_hbm, x_ref, padded_ref, out_ref, arrived, out_copies):
     channels, body = x_hbm.shape[0:2]
     length = taps_ref.shape[1]
+    parts = out_copies.shape[0]
+    size = body // parts
+    ends = [0] + [size * (h + 1) + SUBLANES for h in range(parts - 1)] + [body]
     copies = [
-        pltpu.make_async_copy(x_hbm.at[c], x_ref.at[c, pl.ds(SUBLANES, body), :], arrived.at[c])
-        for c in range(channels)
+        pltpu.make_async_copy(
+            x_hbm.at[:, pl.ds(ends[h], ends[h + 1] - ends[h]), :],
+            x_ref.at[:, pl.ds(SUBLANES + ends[h], ends[h + 1] - ends[h]), :],
+            arrived.at[h],
+        )
+        for h in range(parts)
     ]
     for copy in copies:
         copy.start()
     padded_ref[...] = jnp.zeros(padded_ref.shape, F32)
     padded_ref[:, 0:length] = taps_ref[...]
     edge = jnp.zeros((SUBLANES, LANES), F32)
-    filtered = []
+    tables = []
     for c in range(channels):
         x_ref[c, 0:SUBLANES, :] = edge
         x_ref[c, SUBLANES + body : 2 * SUBLANES + body, :] = edge
         rolled = shifted_copies(padded_ref[c : c + 1, :], LANES, padded_ref.shape[1], 0)
-        table = halves(rolled[:, 0 : 3 * LANES])
-        copies[c].wait()
-        first = SUBLANES - rows
-        near = [x_ref[c, first + rows * k : first + rows * k + body, :] for k in range(3)]
-        filtered.append(dot_of_halves(halves(jnp.concatenate(near, axis=1)), table, ((1,), (1,))))
-    packed = blocks_transposed(filtered, range(channels))
-    for q, value in enumerate(packed):
-        for t in range(body // rows):
-            at = rows * (channels * t + q)
-            out_ref[at : at + rows, :] = value[rows * t : rows * (t + 1), :]
+        tables.append(halves(rolled[:, 0 : 3 * LANES]))
+    first = SUBLANES - rows
+    leaving = []
+    for h in range(parts):
+        filtered = []
+        copies[h].wait()
+        for c in range(channels):
+            near = [x_ref[c, pl.ds(first + rows * k + size * h, size), :] for k in range(3)]
+            filtered.append(dot_of_halves(halves(jnp.concatenate(near, axis=1)), tables[c], ((1,), (1,))))
+        packed = blocks_transposed(filtered, range(channels))
+        for q, value in enumerate(packed):
+            for t in range(size // rows):
+                at = rows * (channels * t + q) + channels * size * h
+                out_ref[at : at + rows, :] = value[rows * t : rows * (t + 1), :]
+        piece = pl.ds(channels * size * h, channels * size)
+        leaving.append(pltpu.make_async_copy(out_ref.at[piece], out_hbm.at[piece], out_copies.at[h]))
+        leaving[-1].start()
+    for copy in leaving:
+        copy.wait()
 
 
 def tables_kernel(taps_ref, mix_ref, high_ref, low_ref, wide_mix_ref, padded_ref):
@@ -198,13 +215,15 @@
     by_tile = slide_region.reshape(channels, rows, tiles, LANES).transpose(0, 2, 1, 3).reshape(stacked)
     packed = pl.pallas_call(
         lambda *refs: across_kernel(rows, *refs),
-        out_shape=flat,
+        out_shape=pltpu.HBM(flat.shape, F32),
         in_specs=[IN_HBM, pl.BlockSpec()],
-        out_specs=IN_VMEM,
+        out_specs=IN_HBM,
         scratch_shapes=[
             scratch((channels, tiles * rows + 2 * SUBLANES, LANES), F32),
             scratch((channels, 4 * LANES), F32),
-            pltpu.SemaphoreType.DMA((channels,)),
+            scratch(flat.shape, F32),
+            pltpu.SemaphoreType.DMA((PARTS,)),
+            pltpu.SemaphoreType.DMA((PARTS,)),
         ],
         compiler_params=SMALL,
         name="across",

time: 198 us -> 198 us (level)
  no operation moved by 1% of the time
where the time goes in v4:
time: 198 us; the launch traced here: 197 us
  blocking collectives  74.8 us (38%)
  waiting for transfers between devices  56.2 us (28%)
  starting transfers between devices  55.7 us (28%)
  Pallas kernels  10.5 us (5%)
    all_to_all x1, blocking collectives, exchanged(): moved = lax.all_to_all(parts, EVERYONE, 0, 0, tiled=True)  74.8 us
    all_to_all x1, waiting for transfers between devices, exchanged(): moved = lax.all_to_all(parts, EVERYONE, 0, 0, tiled=True)  56.2 us
    all_to_all x1, starting transfers between devices, exchanged(): moved = lax.all_to_all(parts, EVERYONE, 0, 0, tiled=True)  55.7 us
  transfers between devices with their start and end apart: 1, of which 1 were waited for; matrix products, arithmetic and copies ran while one was open for 0% of the time, Pallas kernels for 2%

profile of v4, /device:TPU:33, one launch (start us, length us, event | category | flops | bytes accessed | tf_op | source)
XLA Modules:
  0.0 197.4 jit_solution(12812358810263501125)
XLA Ops:
  0.0 3.5 %across.1 = f32[1024,128]{1,0:T(8,128)} custom-call(f32[4,256,128]{2,1,0:T(8,128)} %bitcast.18, f32[4,257]{1,0:T(4,128)} %refs_1_.1), custom_call_target="tpu_custom_call" | custom-call | tf_op jit(solution)/shard_map/across/pallas_call | solution.py:216
  3.5 55.7 %all-to-all-start = ((f32[256,4,128]{2,1,0:T(4,128)}), f32[256,4,128]{2,1,0:T(4,128)S(1)}, u32[]{:S(2)}, u32[]{:S(2)}) async-start(f32[256,4,128]{2,1,0:T(4,128)} %bitcast.17), calls=%async_computation | async-start | bytes 1048576 | tf_op jit(solution)/shard_map/all_to_all | solution.py:248
  59.2 3.5 %tables.1 = (bf16[4,128,1536]{2,1,0:T(8,128)(2,1)S(1)}, bf16[4,128,1536]{2,1,0:T(8,128)(2,1)}, bf16[2,512,512]{2,1,0:T(8,128)(2,1)S(1)}) custom-call(f32[16,257]{1,0:T(8,128)} %taps_ref.1, f32[16,16]{1,0:T(8,128)} %mix_ref.1), custom_call_target="tpu_custom_call" | custom-call | tf_op jit(solution)/shard_map/tables/pallas_call | solution.py:232
  62.7 56.2 %all-to-all-done = f32[256,4,128]{2,1,0:T(4,128)S(1)} async-done(((f32[256,4,128]{2,1,0:T(4,128)}), f32[256,4,128]{2,1,0:T(4,128)S(1)}, u32[]{:S(2)}, u32[]{:S(2)}) %all-to-all-start) | async-done | bytes 524320 | tf_op jit(solution)/shard_map/all_to_all | solution.py:248
  118.9 2.4 %vertical.1 = f32[1024,128]{1,0:T(8,128)S(1)} custom-call(f32[1024,128]{1,0:T(8,128)S(1)} %bitcast.14, bf16[4,128,1536]{2,1,0:T(8,128)(2,1)S(1)} %get-tuple-element.8.refs_1_, bf16[4,128,1536]{2,1,0:T(8,128)(2,1)} %get-tuple-element.9.refs_2_, bf16[2,512,512]{2,1,0:T(8,128)(2,1)S(1)} %get-tuple-element.10.refs_3_), custom_call_target="tpu_custom_call" | custom-call | tf_op jit(solution)/shard_map/vertical/pallas_call | solution.py:251
  121.3 74.8 %all_to_all.10 = f32[256,4,128]{2,1,0:T(4,128)S(1)} all-to-all(f32[256,4,128]{2,1,0:T(4,128)S(1)} %bitcast.15), channel_id=1, replica_groups=mesh['groups'=2,'band_0'=32,'band_1'=2,'chan'=4] {'band_0','band_1','chan'}, dimensions={0} | all-to-all | bytes 1048576 | tf_op jit(solution)/shard_map/all_to_all | solution.py:248
  196.1 1.2 unpack.1
Async XLA Ops:
  3.5 115.4 %all-to-all-start = ((f32[256,4,128]{2,1,0:T(4,128)}), f32[256,4,128]{2,1,0:T(4,128)S(1)}, u32[]{:S(2)}, u32[]{:S(2)}) async-start(f32[256,4,128]{2,1,0:T(4,128)} %bitcast.17), calls=%async_computation | async-start | bytes 1048576 | tf_op jit(solution)/shard_map/all_to_all | solution.py:248
